TPU v7x, 512 devices: a whole 4x8x8 slice. The times are simulated.
512 devices in a mesh: seq: 64 (over y, z_hi, core), tp: 8 (over x, z_lo).
Axes of the slice: x: 4, y: 8, z: 8 (z_hi: 4, z_lo: 2; z = z_hi * 2 + z_lo), core: 2. Of those that a mesh axis runs over, the one named last changes fastest.
Arguments:
- rollout_rows: bfloat16 [24576, 5120], P('seq', 'tp'), may hold values from -6 to 6
- live_rows: int32 [64], P('seq'), may hold values from 129 to 383, as said below
- doc_lengths: int32 [32], replicated, may hold values from 1 to 769, 16384 in all
- block_owner: int32 [64], replicated, may hold values from 0 to 63, each once
- norm_gain: bfloat16 [5120], replicated, may hold values from 0.099609375 to 1.8984375
- qkv_weight: bfloat16 [5120, 5120], P('seq', 'tp'), may hold values from -1.8168052 to 1.8168052
- out_weight: bfloat16 [5120, 3072], P('seq', 'tp'), may hold values from -0.109375 to 0.109375
Outputs:
- layer_out: bfloat16 [16384, 5120], P('seq', 'tp')
- key_cache: bfloat16 [16384, 1024], P('seq', 'tp')
- value_cache: bfloat16 [16384, 1024], P('seq', 'tp')
Inputs may be any that keep to these rules, and one draw needn't show every extreme that they name: Device s's live rows number live_rows[s]; the live rows of the devices before s number at least 256 * s and less than 256 * s + 128; all live rows together number 16384. `block_owner`: a permutation.
All inputs are finite; a program needn't handle non-finite values.
Results may differ from a plain program's by a relative error of at most 0.015.
The roundings to bfloat16 on the way count: a program that leaves them out, or rounds other values in their place, can miss the bound.
Values may be sent and summed in bfloat16 or wider, within the bound.
A program may use at most 64 MiB of HBM per device.

v0:
```python
import jax
import jax.numpy as jnp
from jax import lax
from jax.sharding import PartitionSpec as P

D = 5120
KV_HEADS = 8
HD = 128
HEADS = 24
WINDOW = 4
TOK_DEV = 256


EPSILON = 1e-06
NEG_LARGE = -1e30


def from_everyone(x, axis):
    copies = jnp.broadcast_to(x, (lax.axis_size(axis), *x.shape))
    return lax.all_to_all(copies, axis, split_axis=0, concat_axis=0, tiled=True)


def combined_pairwise(pieces, combine):
    while len(jax.tree.leaves(pieces)[0]) > 1:
        pieces = jax.vmap(combine)(*(pieces[side::2] for side in (0, 1)))
    return pieces[0]


def carried_in(x, axis, combine, identity):
    count, position = (lax.axis_size(axis), lax.axis_index(axis))
    passed = jnp.arange(count) < position

    def kept(part, zero, own):
        part = jnp.where(
            passed.reshape(-1, *(1 for _ in own.shape)), part, jnp.asarray(zero, own.dtype)
        )
        return part

    pieces = from_everyone(x, axis)
    return combined_pairwise(kept(pieces, identity, x), combine)


def shifted(x, axis, by):
    count = lax.axis_size(axis)
    pairs = [(i, i + by) for i in range(count) if 0 <= i + by < count]
    return lax.ppermute(x, axis, pairs)


def in_order(pieces, dim):
    pieces = jnp.moveaxis(pieces, 0, dim)
    dims = pieces.shape
    return pieces.reshape(*dims[:dim], dims[dim] * dims[dim + 1], *dims[dim + 2 :])


def collect(x, axis, dim):
    return in_order(from_everyone(x, axis), dim)


def sent_together(arrays, axis, dim, along):
    both = jnp.concatenate(arrays, axis=along)
    whole, at, done = (lax.all_gather(both, axis, axis=dim, tiled=True), 0, [])
    for a in arrays:
        done.append(lax.slice_in_dim(whole, at, at + a.shape[along], axis=along))
        at += a.shape[along]
    return tuple(done)


def in_blocks(x, dim, count):
    dims = x.shape
    pieces = x.reshape(*dims[:dim], count, dims[dim] // count, *dims[dim + 1 :])
    return jnp.moveaxis(pieces, dim, 0)


def sent_and_summed(x, axis, dim):
    pieces = in_blocks(x, dim, lax.axis_size(axis))
    arrived = lax.all_to_all(pieces, axis, split_axis=0, concat_axis=0, tiled=True)
    return arrived.astype(jnp.float32).sum(axis=0)


def body(rollout_rows, live_rows, doc_lengths, block_owner, norm_gain, qkv_weight, out_weight):
    half_rows = TOK_DEV // 2
    seq_index = lax.axis_index("seq")

    def combine(earlier, later):
        return earlier + later

    before = carried_in(live_rows, "seq", combine, jnp.zeros_like(live_rows))
    spilled_in = before[0] - seq_index * TOK_DEV
    tail_rows = lax.dynamic_slice_in_dim(rollout_rows, live_rows[0] - half_rows, half_rows, 0)
    arrived = shifted(tail_rows, "seq", 1)
    joined = jnp.concatenate([arrived, rollout_rows], 0)
    owned = lax.dynamic_slice_in_dim(joined, half_rows - spilled_in, TOK_DEV, 0)
    full_rows = collect(owned, "tp", 1)
    values_f = full_rows.astype(jnp.float32)
    scale = lax.rsqrt(jnp.mean(values_f * values_f, axis=-1, keepdims=True) + EPSILON)
    normed = (values_f * scale * norm_gain.astype(jnp.float32)).astype(jnp.bfloat16)
    block_rows = qkv_weight.shape[0]
    block_count = D // block_rows
    permuted = normed.reshape(TOK_DEV, block_count, block_rows)[:, block_owner, :].reshape(
        TOK_DEV, D
    )
    positions = jnp.arange(block_count, dtype=jnp.int32)
    inverse = jnp.sum(
        jnp.where(block_owner[None, :] == positions[:, None], positions[None, :], 0), axis=1
    )
    pieces = sent_together((qkv_weight, out_weight), "seq", 0, 1)
    stored = pieces[1]
    projected = jnp.dot(permuted, pieces[0], preferred_element_type=jnp.float32)
    group = HEADS // KV_HEADS
    kv_local = projected.shape[1] // ((group + 2) * HD)
    q_width = kv_local * group * HD
    query_rows = (projected[:, :q_width] * HD ** (-0.5)).astype(jnp.bfloat16)
    key_rows = projected[:, q_width : q_width + kv_local * HD].astype(jnp.bfloat16)
    value_rows = projected[:, q_width + kv_local * HD :].astype(jnp.bfloat16)
    queries = query_rows.reshape(TOK_DEV, kv_local, group, HD)
    query_pos = seq_index * TOK_DEV + jnp.arange(TOK_DEV, dtype=jnp.int32)
    doc_starts = jnp.cumsum(doc_lengths) - doc_lengths
    first_pos = jnp.max(
        jnp.where(doc_starts[None, :] <= query_pos[:, None], doc_starts[None, :], 0), axis=1
    )
    initial = (
        jnp.full((kv_local, group, TOK_DEV), NEG_LARGE, jnp.float32),
        jnp.zeros((kv_local, group, TOK_DEV), jnp.float32),
        jnp.zeros((kv_local, group, TOK_DEV, HD), jnp.float32),
    )
    keys_all, values_all = (key_rows, value_rows)
    for level in range(WINDOW.bit_length() - 1):
        got_keys, got_values = shifted((keys_all, values_all), "seq", 1 << level)
        keys_all = jnp.concatenate([got_keys, keys_all], 0)
        values_all = jnp.concatenate([got_values, values_all], 0)
    state = initial
    for block in range(WINDOW):
        keys_block = keys_all[block * TOK_DEV : (block + 1) * TOK_DEV]
        attend_best, attend_totals, attend_accum = state
        key_count = keys_block.shape[0]
        keys_three = keys_block.reshape(key_count, kv_local, HD)
        values_three = values_all[block * TOK_DEV : (block + 1) * TOK_DEV].reshape(
            key_count, kv_local, HD
        )
        scores = jnp.einsum(
            "tgjd,sgd->gjts", queries, keys_three, preferred_element_type=jnp.float32
        )
        key_pos = (seq_index - WINDOW + 1 + block) * TOK_DEV + jnp.arange(
            key_count, dtype=jnp.int32
        )
        allowed = (key_pos[None, :] <= query_pos[:, None]) & (
            key_pos[None, :] >= first_pos[:, None]
        )
        masked = jnp.where(allowed, scores, NEG_LARGE)
        newest = jnp.maximum(attend_best, jnp.max(masked, axis=-1))
        rescale = jnp.exp(attend_best - newest)
        weights = jnp.where(allowed, jnp.exp(masked - newest[..., None]), 0.0)
        attend_totals = attend_totals * rescale + jnp.sum(weights, axis=-1)
        update = jnp.einsum(
            "gjts,sgd->gjtd",
            weights.astype(jnp.bfloat16),
            values_three,
            preferred_element_type=jnp.float32,
        )
        attend_accum = attend_accum * rescale[..., None] + update
        state = (newest, attend_totals, attend_accum)
    best, totals, accum = state
    context = (
        jnp.transpose(accum / totals[..., None], (2, 0, 1, 3))
        .reshape(TOK_DEV, q_width)
        .astype(jnp.bfloat16)
    )
    delivered = lax.dot_general(
        context, stored, (((1,), (1,)), ((), ())), preferred_element_type=jnp.float32
    )
    partial_value = delivered.reshape(TOK_DEV, block_count, block_rows)[:, inverse, :].reshape(
        TOK_DEV, D
    )
    mixed = sent_and_summed(
        partial_value.astype(jnp.bfloat16).astype(jnp.float32).astype(jnp.bfloat16), "tp", 1
    )
    return (mixed.astype(jnp.bfloat16), key_rows, value_rows)


def solution(mesh):
    in_specs = (P("seq", "tp"), P("seq"), P(), P(), P(), P("seq", "tp"), P("seq", "tp"))
    out_specs = (P("seq", "tp"), P("seq", "tp"), P("seq", "tp"))
    return jax.shard_map(body, mesh=mesh, in_specs=in_specs, out_specs=out_specs, check_vma=False)
```

profile of v0, /device:TPU:1, one launch (start us, length us, event | category | flops | bytes accessed | tf_op | source)
XLA Modules:
  0.0 208.5 jit_solution(18429391535371961624)
XLA Ops:
  7.2 1.6 pad_maximum_fusion
  10.1 17.6 %all-to-all-start = ((s32[64,1,1]{2,1,0:T(1,128)}), s32[64,1,1]{2,1,0:T(1,128)S(1)}, u32[]{:S(2)}, u32[]{:S(2)}) async-start(s32[64,1,1]{2,1,0:T(1,128)} %broadcast_in_dim.109), calls=%async_computation | async-start | bytes 65536 | tf_op jit(solution)/shard_map/all_to_all | solution.py:20
  27.8 1.0 constant_dynamic-slice_fusion
  28.7 4.4 %collective-permute-start = (bf16[128,640]{1,0:T(8,128)(2,1)S(1)}, bf16[128,640]{1,0:T(8,128)(2,1)S(1)}, u32[]{:S(2)}, u32[]{:S(2)}) collective-permute-start(bf16[128,640]{1,0:T(8,128)(2,1)S(1)} %constant_dynamic-slice_fusion), channel_id=1, source_target_pairs={{0,8},{8,16},{16,24},{24,32},{32,40},{40,48},{48,56},{56,64},{64,7... | collective-permute-start | bytes 491528 | tf_op jit(solution)/shard_map/ppermute | solution.py:46
  33.2 6.3 %all-to-all-done = s32[64,1,1]{2,1,0:T(1,128)S(1)} async-done(((s32[64,1,1]{2,1,0:T(1,128)}), s32[64,1,1]{2,1,0:T(1,128)S(1)}, u32[]{:S(2)}, u32[]{:S(2)}) %all-to-all-start) | async-done | bytes 288 | tf_op jit(solution)/shard_map/all_to_all | solution.py:20
  39.5 1.2 reduce.12
  43.7 1.1 fusion.46
  45.1 1.7 broadcast_in_dim.111
  46.8 5.1 %all-to-all-start.1 = ((bf16[8,256,640]{1,2,0:T(8,128)(2,1)}), bf16[8,256,640]{1,2,0:T(8,128)(2,1)S(1)}, u32[]{:S(2)}, u32[]{:S(2)}) async-start(bf16[8,256,640]{1,2,0:T(8,128)(2,1)} %broadcast_in_dim.111), calls=%async_computation.1 | async-start | bytes 5242880 | tf_op jit(solution)/shard_map/all_to_all | solution.py:20
  52.8 47.1 %all-to-all-done.1 = bf16[8,256,640]{1,2,0:T(8,128)(2,1)S(1)} async-done(((bf16[8,256,640]{1,2,0:T(8,128)(2,1)}), bf16[8,256,640]{1,2,0:T(8,128)(2,1)S(1)}, u32[]{:S(2)}, u32[]{:S(2)}) %all-to-all-start.1) | async-done | bytes 2621472 | tf_op jit(solution)/shard_map/all_to_all | solution.py:20
  100.4 0.7 multiply_reduce_fusion
  101.1 0.9 multiply_convert_fusion
  102.0 2.2 %gather_fusion = bf16[64,256,80]{1,2,0:T(8,128)(2,1)} fusion(bf16[256,64,80]{0,2,1:T(8,128)(2,1)S(1)} %multiply_convert_fusion, s32[1024]{0:T(1024)S(1)} %pad_clamp_fusion.1), kind=kCustom, calls=%fused_computation | custom fusion | bytes 5243136 | tf_op jit(solution)/shard_map/gather | solution.py:99
  104.2 30.6 %all-gather.2.cloned.1.call-done = bf16[5120,1024]{1,0:T(8,128)(2,1)} async-done(((bf16[80,1024]{1,0:T(8,128)(2,1)}), bf16[5120,1024]{1,0:T(8,128)(2,1)}) %all-gather.2.cloned.1.call-update) | async-done | bytes 10485776 | tf_op jit(solution)/shard_map/all_gather | solution.py:61
  134.8 5.9 %fusion.61 = (bf16[256,640]{1,0:T(8,128)(2,1)S(1)}, f32[256,640]{1,0:T(8,128)S(1)}) fusion(bf16[256,5120]{0,1:T(8,128)(2,1)} %bitcast.110, bf16[5120,1024]{1,0:T(8,128)(2,1)} %all-gather.2.cloned.1.call-done), kind=kOutput, calls=%fused_computation.103 | convolution fusion | flops 1677885440 | bytes 10158080 | tf_op jit(solution)/shard_map/dot_general | solution.py:108
  140.7 3.7 %collective-permute-start.1 = (bf16[256,128]{1,0:T(8,128)(2,1)S(1)}, bf16[256,128]{1,0:T(8,128)(2,1)S(1)}, u32[]{:S(2)}, u32[]{:S(2)}) collective-permute-start(bf16[256,128]{1,0:T(8,128)(2,1)S(1)} %get-tuple-element.20), channel_id=1, source_target_pairs={{0,8},{8,16},{16,24},{24,32},{32,40},{40,48},{48,56},{56,64},{64,7... | collective-permute-start | bytes 196616 | tf_op jit(solution)/shard_map/ppermute | solution.py:46
  144.6 2.1 %collective-permute-start.3 = (bf16[256,128]{1,0:T(8,128)(2,1)S(1)}, bf16[256,128]{1,0:T(8,128)(2,1)S(1)}, u32[]{:S(2)}, u32[]{:S(2)}) collective-permute-start(bf16[256,128]{1,0:T(8,128)(2,1)S(1)} %get-tuple-element.19), channel_id=1, source_target_pairs={{0,8},{8,16},{16,24},{24,32},{32,40},{40,48},{48,56},{56,64},{64,7... | collective-permute-start | bytes 196616 | tf_op jit(solution)/shard_map/ppermute | solution.py:46
  147.0 4.3 %collective-permute-start.2 = (bf16[512,128]{1,0:T(8,128)(2,1)S(1)}, bf16[512,128]{1,0:T(8,128)(2,1)S(1)}, u32[]{:S(2)}, u32[]{:S(2)}) collective-permute-start(bf16[512,128]{1,0:T(8,128)(2,1)S(1)} %pad_maximum_fusion.1), channel_id=1, source_target_pairs={{0,16},{8,24},{16,32},{24,40},{32,48},{40,56},{48,64},{56,72},{64,... | collective-permute-start | bytes 393224 | tf_op jit(solution)/shard_map/ppermute | solution.py:46
  151.4 3.7 %collective-permute-start.4 = (bf16[512,128]{1,0:T(8,128)(2,1)S(1)}, bf16[512,128]{1,0:T(8,128)(2,1)S(1)}, u32[]{:S(2)}, u32[]{:S(2)}) collective-permute-start(bf16[512,128]{1,0:T(8,128)(2,1)S(1)} %pad_maximum_fusion.2), channel_id=1, source_target_pairs={{0,16},{8,24},{16,32},{24,40},{32,48},{40,56},{48,64},{56,72},{64,... | collective-permute-start | bytes 393224 | tf_op jit(solution)/shard_map/ppermute | solution.py:46
  157.8 0.9 slice-done
  158.6 1.5 fusion.66
  160.1 2.2 %gather_fusion.1 = bf16[64,256,80]{1,2,0:T(8,128)(2,1)} fusion(bf16[256,64,80]{0,2,1:T(8,128)(2,1)S(1)} %fusion.66, s32[1024]{0:T(1024)S(1)} %pad_clamp_fusion), kind=kCustom, calls=%fused_computation.1 | custom fusion | bytes 5243136 | tf_op jit(solution)/shard_map/gather | solution.py:171
  162.4 37.9 %all_to_all.19 = bf16[8,256,640]{1,2,0:T(8,128)(2,1)S(1)} all-to-all(bf16[8,256,640]{1,2,0:T(8,128)(2,1)} %bitcast.109), channel_id=1, replica_groups=mesh['seq'=64,'tp'=8] {'tp'}, dimensions={0} | all-to-all | bytes 5242880 | tf_op jit(solution)/shard_map/all_to_all | solution.py:76
  200.8 0.9 copy.90
  (73 shorter events, 7.6 us)
Async XLA Ops:
  7.2 127.6 %all-gather.2.cloned.1.call-start = ((), (), s32[]{:S(2)}) async-start(), calls=%async_computation.3 | async-start | bytes 10649600 | tf_op jit(solution)/shard_map/all_gather | solution.py:61
  10.1 29.4 %all-to-all-start = ((s32[64,1,1]{2,1,0:T(1,128)}), s32[64,1,1]{2,1,0:T(1,128)S(1)}, u32[]{:S(2)}, u32[]{:S(2)}) async-start(s32[64,1,1]{2,1,0:T(1,128)} %broadcast_in_dim.109), calls=%async_computation | async-start | bytes 65536 | tf_op jit(solution)/shard_map/all_to_all | solution.py:20
  28.7 15.0 %collective-permute-start = (bf16[128,640]{1,0:T(8,128)(2,1)S(1)}, bf16[128,640]{1,0:T(8,128)(2,1)S(1)}, u32[]{:S(2)}, u32[]{:S(2)}) collective-permute-start(bf16[128,640]{1,0:T(8,128)(2,1)S(1)} %constant_dynamic-slice_fusion), channel_id=1, source_target_pairs={{0,8},{8,16},{16,24},{24,32},{32,40},{40,48},{48,56},{56,64},{64,7... | collective-permute-start | bytes 491528 | tf_op jit(solution)/shard_map/ppermute | solution.py:46
  45.0 6.8 %copy-start.2 = (bf16[5120]{0:T(1024)(128)(2,1)S(1)}, bf16[5120]{0:T(1024)(128)(2,1)}, u32[]{:S(2)}) copy-start(bf16[5120]{0:T(1024)(128)(2,1)} %param.11) | copy-start | bytes 30724
  45.1 6.9 %copy-start.3 = (s32[32]{0:T(128)S(1)}, s32[32]{0:T(128)}, u32[]{:S(2)}) copy-start(s32[32]{0:T(128)} %param.9) | copy-start | bytes 388
  45.1 7.2 %copy-start.4 = (s32[64]{0:T(128)S(1)}, s32[64]{0:T(128)}, u32[]{:S(2)}) copy-start(s32[64]{0:T(128)} %param.10) | copy-start | bytes 772
  46.8 53.1 %all-to-all-start.1 = ((bf16[8,256,640]{1,2,0:T(8,128)(2,1)}), bf16[8,256,640]{1,2,0:T(8,128)(2,1)S(1)}, u32[]{:S(2)}, u32[]{:S(2)}) async-start(bf16[8,256,640]{1,2,0:T(8,128)(2,1)} %broadcast_in_dim.111), calls=%async_computation.1 | async-start | bytes 5242880 | tf_op jit(solution)/shard_map/all_to_all | solution.py:20
  140.7 6.3 %copy-start.1 = (bf16[256,128]{1,0:T(8,128)(2,1)}, bf16[256,128]{1,0:T(8,128)(2,1)S(1)}, u32[]{:S(2)}) copy-start(bf16[256,128]{1,0:T(8,128)(2,1)S(1)} %get-tuple-element.20) | copy-start | bytes 196612
  140.7 15.2 %copy-start = (bf16[256,128]{1,0:T(8,128)(2,1)}, bf16[256,128]{1,0:T(8,128)(2,1)S(1)}, u32[]{:S(2)}) copy-start(bf16[256,128]{1,0:T(8,128)(2,1)S(1)} %get-tuple-element.19) | copy-start | bytes 196612
  140.7 6.3 %collective-permute-start.1 = (bf16[256,128]{1,0:T(8,128)(2,1)S(1)}, bf16[256,128]{1,0:T(8,128)(2,1)S(1)}, u32[]{:S(2)}, u32[]{:S(2)}) collective-permute-start(bf16[256,128]{1,0:T(8,128)(2,1)S(1)} %get-tuple-element.20), channel_id=1, source_target_pairs={{0,8},{8,16},{16,24},{24,32},{32,40},{40,48},{48,56},{56,64},{64,7... | collective-permute-start | bytes 196616 | tf_op jit(solution)/shard_map/ppermute | solution.py:46
  144.6 6.8 %collective-permute-start.3 = (bf16[256,128]{1,0:T(8,128)(2,1)S(1)}, bf16[256,128]{1,0:T(8,128)(2,1)S(1)}, u32[]{:S(2)}, u32[]{:S(2)}) collective-permute-start(bf16[256,128]{1,0:T(8,128)(2,1)S(1)} %get-tuple-element.19), channel_id=1, source_target_pairs={{0,8},{8,16},{16,24},{24,32},{32,40},{40,48},{48,56},{56,64},{64,7... | collective-permute-start | bytes 196616 | tf_op jit(solution)/shard_map/ppermute | solution.py:46
  147.0 8.3 %collective-permute-start.2 = (bf16[512,128]{1,0:T(8,128)(2,1)S(1)}, bf16[512,128]{1,0:T(8,128)(2,1)S(1)}, u32[]{:S(2)}, u32[]{:S(2)}) collective-permute-start(bf16[512,128]{1,0:T(8,128)(2,1)S(1)} %pad_maximum_fusion.1), channel_id=1, source_target_pairs={{0,16},{8,24},{16,32},{24,40},{32,48},{40,56},{48,64},{56,72},{64,... | collective-permute-start | bytes 393224 | tf_op jit(solution)/shard_map/ppermute | solution.py:46
  151.4 5.8 %collective-permute-start.4 = (bf16[512,128]{1,0:T(8,128)(2,1)S(1)}, bf16[512,128]{1,0:T(8,128)(2,1)S(1)}, u32[]{:S(2)}, u32[]{:S(2)}) collective-permute-start(bf16[512,128]{1,0:T(8,128)(2,1)S(1)} %pad_maximum_fusion.2), channel_id=1, source_target_pairs={{0,16},{8,24},{16,32},{24,40},{32,48},{40,56},{48,64},{56,72},{64,... | collective-permute-start | bytes 393224 | tf_op jit(solution)/shard_map/ppermute | solution.py:46
  156.5 2.1 %slice-start = ((bf16[5120,1024]{1,0:T(8,128)(2,1)}), bf16[5120,384]{1,0:T(8,128)(2,1)S(1)}, s32[]{:S(2)}) async-start(bf16[5120,1024]{1,0:T(8,128)(2,1)} %all-gather.2.cloned.1.call-done), calls=%async_computation.4 | async-start | bytes 7864320 | tf_op jit(solution)/shard_map/slice | solution.py:63
Sparse Core Ops, SparseCore 0:
  11.8 122.8 all-gather.1
where the time goes:
time: 212 us; the launch traced here: 209 us
  waiting for transfers between devices  84 us (40%)
  starting transfers between devices  41 us (19%)
  blocking collectives  37.9 us (18%)
  between operations  16.4 us (8%)
  local copies, waits for them, and re-layouts  11.7 us (6%)
  matrix products  9.61 us (5%)
  other arithmetic  8.02 us (4%)
    all_to_all x2, waiting for transfers between devices, from_everyone(): return lax.all_to_all(copies, axis, split_axis=0, concat_axis=0, tiled=True)  53.4 us
    all_to_all x1, blocking collectives, sent_and_summed(): lax.all_to_all(pieces, axis, split_axis=0, concat_axis=0, tiled=True)  37.9 us
    all_gather x1, waiting for transfers between devices, sent_together(): whole, at, done = (lax.all_gather(both, axis, axis=dim, tiled=True), 0, [])  30.6 us
    all_to_all x2, starting transfers between devices, from_everyone(): return lax.all_to_all(copies, axis, split_axis=0, concat_axis=0, tiled=True)  22.7 us
    ppermute x5, starting transfers between devices, shifted(): return lax.ppermute(x, axis, pairs)  18.2 us
    dot_general x1, matrix products, body(): projected = jnp.dot(permuted, pieces[0], preferred_element_type=jnp.float32)  5.89 us
  transfers between devices with their start and end apart: 8, of which 3 were waited for; matrix products, arithmetic and copies ran while one was open for 7% of the time, Pallas kernels for 0%

commit v1 on v0

v1 whole, which is shorter than its diff:
```python
import jax
import jax.numpy as jnp
from jax import lax
from jax.experimental import pallas as pl
from jax.experimental.pallas import tpu as pltpu
from jax.sharding import PartitionSpec as P

D = 5120
HD = 128
GROUP = 3
TOK = 256
HALF = 128
CAP = 384
BLK = 80
N_SEQ = 64
N_TP = 8
N_Y, N_Z, N_X = 8, 4, 4
COLS = 640
QW = GROUP * HD
EPSILON = 1e-06
NEG = -1e30
N_COPIES = 176
MESH = pl.DeviceIdType.MESH
BF = jnp.bfloat16
F32 = jnp.float32


def kernel(
    live_s, docs_s, slot_s, gain_v, roll_h, wq_h, wo_h,
    out_ref, key_ref, value_ref,
    rows, wq, wo, acts, tail_s, tail_r, live_own, live_p, live_z, live_y, ssq,
    acc, kv_own, kv_in, bias, ctx, part_s, part_r,
    local_sem, send_sem, recv_sem,
):
    seq = lax.axis_index("seq")
    tp = lax.axis_index("tp")
    core = lax.rem(seq, 2)
    zh = lax.rem(lax.div(seq, 2), N_Z)
    y = lax.div(seq, 2 * N_Z)
    zl = lax.rem(tp, 2)
    x = lax.div(tp, 2)
    d = 1 - 2 * core

    def wrap_y(v):
        return lax.rem(v + 2 * N_Y, N_Y)

    def wrap_z(v):
        return lax.rem(v + 2 * N_Z, N_Z)

    def wrap_x(v):
        return lax.rem(v + 2 * N_X, N_X)

    def at_seq(y_, z_, c_):
        return ((y_ * N_Z + z_) * 2 + c_, tp)

    def at_tp(x_, zl_):
        return (seq, x_ * 2 + zl_)

    def slot(y_, z_):
        return core * (N_Y * N_Z) + y_ * N_Z + z_

    partner = at_seq(y, zh, 1 - core)
    next_1 = (lax.rem(seq + 1, N_SEQ), tp)
    next_2 = (lax.rem(seq + 2, N_SEQ), tp)
    prev_1 = (lax.rem(seq + N_SEQ - 1, N_SEQ), tp)
    prev_2 = (lax.rem(seq + N_SEQ - 2, N_SEQ), tp)

    started = []

    def send(src, dst, device):
        n = len(started)
        copy = pltpu.make_async_remote_copy(
            src_ref=src, dst_ref=dst, send_sem=send_sem.at[n], recv_sem=recv_sem.at[n],
            device_id=device, device_id_type=MESH,
        )
        copy.start()
        started.append(copy)
        return copy

    load_q = pltpu.make_async_copy(wq_h, wq.at[slot(y, zh)], local_sem.at[0])
    load_o = pltpu.make_async_copy(wo_h, wo.at[slot(y, zh)], local_sem.at[1])
    load_r = pltpu.make_async_copy(roll_h, rows, local_sem.at[2])
    load_q.start()
    load_r.start()
    load_o.start()

    barrier = pltpu.get_barrier_semaphore()
    greeted = [partner, next_1, next_2, prev_1, prev_2]
    greeted += [at_seq(y, wrap_z(zh + k), core) for k in range(1, N_Z)]
    greeted += [at_seq(wrap_y(y + k), zh, core) for k in range(1, N_Y)]
    greeted += [(seq, lax.rem(tp + k, N_TP)) for k in range(1, N_TP)]
    for device in greeted:
        pl.semaphore_signal(barrier, inc=1, device_id=device, device_id_type=MESH)
    live_own[...] = jnp.full((8, 128), live_s[0], jnp.int32)
    gain_rows = gain_v[...].astype(F32)
    picked = lax.broadcasted_iota(jnp.int32, (N_TP, COLS), 0) == tp
    gain = jnp.sum(jnp.where(picked, gain_rows, 0.0), axis=0, keepdims=True)
    load_q.wait()
    load_r.wait()
    pl.semaphore_wait(barrier, len(greeted))

    up_z = at_seq(y, wrap_z(zh + d), core)
    down_z = at_seq(y, wrap_z(zh - d), core)
    up_y = at_seq(wrap_y(y + d), zh, core)
    down_y = at_seq(wrap_y(y - d), zh, core)

    def z_own(buf):
        own = buf.at[slot(y, zh)]
        return send(own, own, up_z), send(own, own, down_z)

    def z_on(buf):
        held = buf.at[slot(y, wrap_z(zh - d))]
        return send(held, held, up_z)

    z_blocks = [zh, wrap_z(zh - d), wrap_z(zh + d), wrap_z(zh + 2 * d)]

    def ring_up(buf, b, k):
        held = buf.at[slot(wrap_y(y - (k - 1) * d), z_blocks[b])]
        return send(held, held, up_y)

    def ring_down(buf, b, k):
        held = buf.at[slot(wrap_y(y + (k - 1) * d), z_blocks[b])]
        return send(held, held, down_y)

    def across(buf, k):
        held = buf.at[pl.ds(core * (N_Y * N_Z) + wrap_y(y + k * d) * N_Z, N_Z)]
        return send(held, held, partner)

    q_up, q_down = {}, {}
    q_z1, q_z2 = z_own(wq)
    q_up[0, 1], q_down[0, 1] = ring_up(wq, 0, 1), ring_down(wq, 0, 1)

    live_to_partner = send(live_own, live_p, partner)

    def squares(values):
        total = jnp.sum(values * values, axis=1, keepdims=True)
        return jnp.transpose(jnp.broadcast_to(total, (HALF, 128)))[:8]

    own_a = rows[pl.ds(0, HALF), :].astype(F32)
    acts[tp, pl.ds(0, HALF), :] = (own_a * gain).astype(BF)
    x_up = at_tp(wrap_x(x + 1), zl)
    x_down = at_tp(wrap_x(x - 1), zl)
    z_other = at_tp(x, 1 - zl)

    def chunk(x_, zl_, part):
        return acts.at[wrap_x(x_) * 2 + zl_, pl.ds(part * HALF, HALF)]

    def gather_own(part):
        own = chunk(x, zl, part)
        return [send(own, own, z_other), send(own, own, x_up), send(own, own, x_down)]

    def gather_second(part):
        held = chunk(x, 1 - zl, part)
        return [send(held, held, x_up), send(held, held, x_down)]

    def gather_third_up(part):
        held = chunk(x - 1, zl, part)
        return send(held, held, x_up)

    def gather_third_down(part):
        held = chunk(x + 1, 1 - zl, part)
        return send(held, held, x_down)

    a_first = gather_own(0)

    row = lax.broadcasted_iota(jnp.int32, (HALF, CAP), 0)
    col = lax.broadcasted_iota(jnp.int32, (HALF, CAP), 1)
    chosen = (col == row + (live_s[0] - HALF)).astype(BF)
    tail_s[...] = jnp.dot(chosen, rows[...], preferred_element_type=F32).astype(BF)
    tail = send(tail_s, tail_r, next_1)

    ssq[tp, 0] = squares(own_a)

    live_to_partner.wait_recv()
    live_z[0] = live_own[...] + live_p[...]
    live_over_z = [
        send(live_z.at[0], live_z.at[k], at_seq(y, wrap_z(zh + k), core)) for k in range(1, N_Z)
    ]

    position = seq * TOK + lax.broadcasted_iota(jnp.int32, (TOK, 128), 0)
    first = jnp.zeros((TOK, 128), jnp.int32)
    begin = docs_s[0]
    for doc in range(1, 32):
        first = jnp.maximum(first, jnp.where(position >= begin, begin, 0))
        begin = begin + docs_s[doc]
    key_base = [seq, seq - 2, seq - 3 + 2 * core, seq - 1 - 2 * core]
    lane = lax.broadcasted_iota(jnp.int32, (TOK, 128), 1)
    for b in range(4):
        for side in range(2):
            key_pos = key_base[b] * TOK + side * 128 + lane
            allowed = (key_pos <= position) & (key_pos >= first)
            bias[b, :, pl.ds(side * 128, 128)] = jnp.where(allowed, 0.0, NEG)

    q_z1.wait_recv()
    q_z3 = z_on(wq)
    q_up[1, 1], q_down[1, 1] = ring_up(wq, 1, 1), ring_down(wq, 1, 1)
    q_z2.wait_recv()
    q_up[2, 1], q_down[2, 1] = ring_up(wq, 2, 1), ring_down(wq, 2, 1)
    a_first[0].wait_recv()
    a_second = gather_second(0)
    for copy in live_over_z:
        copy.wait_recv()
    live_y[0] = live_z[0] + live_z[1] + live_z[2] + live_z[3]
    live_over_y = [
        send(live_y.at[0], live_y.at[k], at_seq(wrap_y(y + k), zh, core)) for k in range(1, N_Y)
    ]
    q_z3.wait_recv()
    q_up[3, 1], q_down[3, 1] = ring_up(wq, 3, 1), ring_down(wq, 3, 1)
    q_across = [across(wq, 0)]
    a_first[1].wait_recv()
    a_third = [gather_third_up(0)]
    a_second[1].wait_recv()
    a_third.append(gather_third_down(0))

    for copy in live_over_y:
        copy.wait_recv()
    before = live_p[...] * core - seq * TOK
    for k in range(1, N_Z):
        before = before + live_z[k] * (k <= zh).astype(jnp.int32)
    for k in range(1, N_Y):
        before = before + live_y[k] * (k <= y).astype(jnp.int32)
    spilled = before[:1, :]
    tail.wait_recv()
    row_b = lax.broadcasted_iota(jnp.int32, (HALF, 128), 0)
    keep = jnp.broadcast_to((row_b + spilled < HALF)[:, :1], (HALF, COLS))
    own_b = jnp.where(
        keep, rows[pl.ds(HALF, HALF), :].astype(F32), tail_r[...].astype(F32)
    )
    acts[tp, pl.ds(HALF, HALF), :] = (own_b * gain).astype(BF)
    b_first = gather_own(1)
    ssq[tp, 1] = squares(own_b)
    ssq_copies = [
        send(ssq.at[tp], ssq.at[tp], (seq, lax.rem(tp + k, N_TP))) for k in range(1, N_TP)
    ]

    load_o.wait()
    o_up, o_down = {}, {}
    o_z1, o_z2 = z_own(wo)

    def step(buf, up, down, k):
        for b in range(4):
            up[b, k - 1].wait_recv()
            up[b, k] = ring_up(buf, b, k)
            down[b, k - 1].wait_recv()
            if k < 4:
                down[b, k] = ring_down(buf, b, k)
        return [across(buf, -(k - 1)), across(buf, k - 1)]

    q_across += step(wq, q_up, q_down, 2)
    b_first[0].wait_recv()
    b_second = gather_second(1)
    o_z1.wait_recv()
    o_z3 = z_on(wo)
    b_first[1].wait_recv()
    b_third = [gather_third_up(1)]
    b_second[1].wait_recv()
    b_third.append(gather_third_down(1))
    q_across += step(wq, q_up, q_down, 3)
    q_across += step(wq, q_up, q_down, 4)

    o_z2.wait_recv()
    o_z3.wait_recv()
    for b in range(4):
        o_up[b, 1], o_down[b, 1] = ring_up(wo, b, 1), ring_down(wo, b, 1)
    o_across = [across(wo, 0)]

    for b in range(4):
        q_up[b, 4].wait_recv()
    q_across.append(across(wq, 4))
    for copy in a_first[2:] + a_second[:1] + a_third + b_first[2:] + b_second[:1] + b_third:
        copy.wait_recv()
    for copy in ssq_copies:
        copy.wait_recv()
    for copy in q_across:
        copy.wait_recv()

    acc[...] = jnp.zeros_like(acc)

    def project(t, carry):
        blocks = [wq[slot_s[t * 8 + i]] for i in range(8)]
        weight = jnp.concatenate(blocks, axis=0)
        acc[...] += jnp.dot(acts[t], weight, preferred_element_type=F32)
        return carry

    lax.fori_loop(0, N_TP, project, 0)
    o_across += step(wo, o_up, o_down, 2)

    total = ssq[0]
    for t in range(1, N_TP):
        total = total + ssq[t]
    scale_row = lax.rsqrt(total * (1.0 / D) + EPSILON)
    scale = jnp.concatenate(
        [jnp.transpose(jnp.broadcast_to(scale_row[h, :1], (128, 128))) for h in range(2)], axis=0
    )
    turn_row = lax.broadcasted_iota(jnp.int32, (TOK, TOK), 0)
    turn_col = lax.broadcasted_iota(jnp.int32, (TOK, TOK), 1)
    spilled_wide = jnp.concatenate([spilled, spilled], axis=1)
    turn = (((turn_col - turn_row + spilled_wide + TOK) & (TOK - 1)) == 0).astype(BF)

    def in_order(values):
        return jnp.dot(turn, values, preferred_element_type=F32).astype(BF)

    keys = in_order((acc[:, QW : QW + HD] * scale).astype(BF))
    values = in_order((acc[:, QW + HD :] * scale).astype(BF))
    kv_own[:, :HD] = keys
    kv_own[:, HD:] = values
    kv_1 = send(kv_own, kv_in.at[0], next_2)
    n_kv = len(started)

    def kv_copy(src):
        return pltpu.make_async_remote_copy(
            src_ref=src, dst_ref=kv_in.at[1], send_sem=send_sem.at[n_kv],
            recv_sem=recv_sem.at[n_kv], device_id=next_1, device_id_type=MESH,
        )

    @pl.when(core == 0)
    def _():
        kv_copy(kv_own).start()

    kv_2 = kv_copy(kv_own)
    started.append(kv_2)
    key_ref[...] = keys
    value_ref[...] = values
    queries = [
        in_order((acc[:, h * HD : (h + 1) * HD] * scale * HD ** (-0.5)).astype(BF))
        for h in range(GROUP)
    ]
    kv_1.wait_recv()

    @pl.when(core == 1)
    def _():
        kv_copy(kv_in.at[0]).start()

    kv_3 = send(kv_in.at[0], kv_in.at[2], partner)
    o_across += step(wo, o_up, o_down, 3)
    kv_2.wait_recv()
    kv_3.wait_recv()
    o_across += step(wo, o_up, o_down, 4)

    pieces = [kv_own, kv_in.at[0], kv_in.at[1], kv_in.at[2]]
    for h in range(GROUP):
        scores = [
            lax.dot_general(
                queries[h], pieces[b][:, :HD], (((1,), (1,)), ((), ())),
                preferred_element_type=F32,
            ) + bias[b]
            for b in range(4)
        ]
        best = jnp.maximum(
            jnp.maximum(scores[0], scores[1]), jnp.maximum(scores[2], scores[3])
        )
        best = jnp.max(best, axis=1, keepdims=True)
        weights = [jnp.exp(s - best) for s in scores]
        totals = jnp.sum(weights[0] + weights[1] + weights[2] + weights[3], axis=1, keepdims=True)
        summed = jnp.dot(weights[0].astype(BF), pieces[0][:, HD:], preferred_element_type=F32)
        for b in range(1, 4):
            summed = summed + jnp.dot(
                weights[b].astype(BF), pieces[b][:, HD:], preferred_element_type=F32
            )
        ctx[:, h * HD : (h + 1) * HD] = (summed / totals).astype(BF)

    for b in range(4):
        o_up[b, 4].wait_recv()
    o_across.append(across(wo, 4))
    for copy in o_across:
        copy.wait_recv()

    base = len(started)

    def partial_sum(t):
        weight = jnp.concatenate([wo[slot_s[t * 8 + i]] for i in range(8)], axis=0)
        delivered = lax.dot_general(
            ctx[...], weight, (((1,), (1,)), ((), ())), preferred_element_type=F32
        )
        return delivered.astype(BF)

    def part_copy(k):
        t = lax.rem(tp + k, N_TP)
        return pltpu.make_async_remote_copy(
            src_ref=part_s.at[k], dst_ref=part_r.at[k], send_sem=send_sem.at[base + k - 1],
            recv_sem=recv_sem.at[base + k - 1], device_id=(seq, t), device_id_type=MESH,
        )

    def deliver(i, carry):
        k = lax.rem(i + 4, N_TP)
        t = lax.rem(tp + k, N_TP)
        part_s[k] = partial_sum(t)

        @pl.when(k > 0)
        def _():
            part_copy(k).start()

        return carry

    lax.fori_loop(0, N_TP, deliver, 0)

    mixed = part_s[0].astype(F32)
    for k in range(1, N_TP):
        part_copy(k).wait_recv()
        mixed = mixed + part_r[k].astype(F32)
    out_ref[...] = mixed.astype(BF)
    for copy in started:
        copy.wait_send()
    for k in range(1, N_TP):
        part_copy(k).wait_send()


def body(rollout_rows, live_rows, doc_lengths, block_owner, norm_gain, qkv_weight, out_weight):
    positions = jnp.arange(N_SEQ, dtype=jnp.int32)
    slots = lax.rem(positions, 2) * (N_SEQ // 2) + positions // 2
    slot_of = jnp.sum(
        jnp.where(block_owner[None, :] == positions[:, None], slots[None, :], 0), axis=1
    )
    smem = pl.BlockSpec(memory_space=pltpu.SMEM)
    vmem = pl.BlockSpec(memory_space=pltpu.VMEM)
    anyw = pl.BlockSpec(memory_space=pl.ANY)
    V = pltpu.VMEM
    return pl.pallas_call(
        kernel,
        out_shape=(
            jax.ShapeDtypeStruct((TOK, COLS), BF),
            jax.ShapeDtypeStruct((TOK, HD), BF),
            jax.ShapeDtypeStruct((TOK, HD), BF),
        ),
        in_specs=[smem, smem, smem, vmem, anyw, anyw, anyw],
        out_specs=(vmem, vmem, vmem),
        scratch_shapes=[
            V((CAP, COLS), BF),
            V((N_SEQ, BLK, COLS), BF),
            V((N_SEQ, BLK, QW), BF),
            V((N_TP, TOK, COLS), BF),
            V((HALF, COLS), BF),
            V((HALF, COLS), BF),
            V((8, 128), jnp.int32),
            V((8, 128), jnp.int32),
            V((N_Z, 8, 128), jnp.int32),
            V((N_Y, 8, 128), jnp.int32),
            V((N_TP, 2, 8, 128), F32),
            V((TOK, COLS), F32),
            V((TOK, 2 * HD), BF),
            V((3, TOK, 2 * HD), BF),
            V((4, TOK, TOK), F32),
            V((TOK, QW), BF),
            V((N_TP, TOK, COLS), BF),
            V((N_TP, TOK, COLS), BF),
            pltpu.SemaphoreType.DMA((3,)),
            pltpu.SemaphoreType.DMA((N_COPIES,)),
            pltpu.SemaphoreType.DMA((N_COPIES,)),
        ],
        compiler_params=pltpu.CompilerParams(collective_id=0, has_side_effects=True),
    )(
        live_rows, doc_lengths, slot_of, norm_gain.reshape(N_TP, COLS),
        rollout_rows, qkv_weight, out_weight,
    )


def solution(mesh):
    in_specs = (P("seq", "tp"), P("seq"), P(), P(), P(), P("seq", "tp"), P("seq", "tp"))
    out_specs = (P("seq", "tp"), P("seq", "tp"), P("seq", "tp"))
    return jax.shard_map(body, mesh=mesh, in_specs=in_specs, out_specs=out_specs, check_vma=False)
```

time: 212 us -> 141 us (0.67); the launches traced: 209 us -> 141 us
  Pallas kernels: 0 us -> 134 us
  waiting for transfers between devices: 84 us -> 0 us
  starting transfers between devices: 41 us -> 0 us
  blocking collectives: 37.9 us -> 0 us
  between operations: 16.4 us -> 1.31 us
  matrix products: 9.61 us -> 0 us
  other arithmetic: 8.02 us -> 0.63 us
  local copies, waits for them, and re-layouts: 11.7 us -> 5.21 us
    pallas_call x0 -> x1, Pallas kernels: none -> 134 us  [body(): pl.pallas_call(kernel, out_shape=(jax.ShapeDtypeStruct((TOK, COLS), BF),...]
    all_to_all x2 -> x0, waiting for transfers between devices: 53.4 us -> none  [from_everyone(): return lax.all_to_all(copies, axis, split_axis=0, concat_axis=0, tiled=True)]
    all_to_all x1 -> x0, blocking collectives: 37.9 us -> none  [sent_and_summed(): lax.all_to_all(pieces, axis, split_axis=0, concat_axis=0, tiled=True)]
    all_gather x1 -> x0, waiting for transfers between devices: 30.6 us -> none  [sent_together(): whole, at, done = (lax.all_gather(both, axis, axis=dim, tiled=True), 0, [])]
    all_to_all x2 -> x0, starting transfers between devices: 22.7 us -> none  [from_everyone(): return lax.all_to_all(copies, axis, split_axis=0, concat_axis=0, tiled=True)]
    ppermute x5 -> x0, starting transfers between devices: 18.2 us -> none  [shifted(): return lax.ppermute(x, axis, pairs)]
    dot_general x10 -> x0, matrix products: 9.61 us -> none  [the longest x1 5.89 us: body(): projected = jnp.dot(permuted, pieces[0], preferred_element_type=jnp.float32)]
    gather x2 -> x0, local copies, waits for them, and re-layouts: 4.45 us -> none  [the longest x1 2.23 us: body(): normed.reshape(TOK_DEV, block_count, block_rows)[:, block_owner, :]]
  transfers between devices with their start and end apart: 8 -> 0, of which waited for: 3 -> 0; matrix products, arithmetic and copies ran while one was open for 7% -> 0% of each run, Pallas kernels for 0% -> 0%
where the time goes in v1:
time: 141 us
  Pallas kernels  134 us (95%)
  local copies, waits for them, and re-layouts  5.21 us (4%)
    pallas_call x1, Pallas kernels, body(): pl.pallas_call(kernel, out_shape=(jax.ShapeDtypeStruct((TOK, COLS), BF),...  134 us
    unnamed x9, local copies, waits for them, and re-layouts  3.89 us

profile of v1, /device:TPU:1, one launch (start us, length us, event | category | flops | bytes accessed | tf_op | source)
XLA Modules:
  0.0 140.8 jit_solution(2874735155987439919)
XLA Ops:
  1.3 0.0 copy-start.2
  1.3 0.6 copy-done.2
  1.9 0.6 select_reduce_fusion.slot_s
  2.6 1.3 reshape.25.gain_v
  3.9 133.7 %shard_map.94 = (bf16[256,640]{1,0:T(8,128)(2,1)}, bf16[256,128]{1,0:T(8,128)(2,1)}, bf16[256,128]{1,0:T(8,128)(2,1)}) custom-call(s32[1]{0:T(128)S(6)} %copy.13.live_s, s32[32]{0:T(128)} %docs_s.1, s32[64]{0:T(128)} %select_reduce_fusion.slot_s, bf16[8,640]{1,0:T(8,128)(2,1)} %reshape.25.gain_v, bf16[384,640]{1,0:T(8,128)(2,1)} %roll_h.1, ...), custom_call_target="tpu_custom_call" | custom-call | tf_op jit(solution)/shard_map/pallas_call | solution.py:418
  137.6 0.0 copy-start.1
  137.6 1.8 %copy.14 = bf16[256,640]{1,0:T(8,128)(2,1)} copy(bf16[256,640]{1,0:T(8,128)(2,1)} %get-tuple-element.6) | data formatting | bytes 655360
  139.3 0.0 copy-done.1
  139.3 0.0 copy-start
  139.3 0.6 copy.15
  140.0 0.2 copy-done
  140.2 0.6 copy.16
  (1 shorter events, 0.0 us)
Async XLA Ops:
  1.3 0.7 copy-start.2
  137.6 1.8 %copy-start.1 = (bf16[256,128]{1,0:T(8,128)(2,1)S(1)}, bf16[256,128]{1,0:T(8,128)(2,1)}, u32[]{:S(2)}) copy-start(bf16[256,128]{1,0:T(8,128)(2,1)} %get-tuple-element.7) | copy-start | bytes 196612
  139.3 0.9 copy-start

commit v2 on v1

v2 whole, which is shorter than its diff:
```python
import jax
import jax.numpy as jnp
from jax import lax
from jax.experimental import pallas as pl
from jax.experimental.pallas import tpu as pltpu
from jax.sharding import PartitionSpec as P

D = 5120
HD = 128
GROUP = 3
TOK = 256
HALF = 128
CAP = 384
BLK = 80
N_SEQ = 64
N_TP = 8
N_Y, N_Z, N_X = 8, 4, 4
COLS = 640
QW = GROUP * HD
EPSILON = 1e-06
NEG = -1e30
N_COPIES = 200
O_FIRST = 48
R1 = 112
MESH = pl.DeviceIdType.MESH
BF = jnp.bfloat16
F32 = jnp.float32


def kernel(
    live_s, docs_s, slot_s, gain_v, roll_h, wqkv_h, wo_h,
    out_ref, key_ref, value_ref,
    rows, wkv, wq, wo, acts, tail_s, tail_r, live_own, live_p, live_z, live_y, ssq,
    acc_kv, acc_q, kv_own, kv_in, bias, ctx, part,
    z1_r, pair_s, x1_r, x2_r, sum2_s, z2_s, z2_r,
    local_sem, send_sem, recv_sem,
):
    seq = lax.axis_index("seq")
    tp = lax.axis_index("tp")
    core = lax.rem(seq, 2)
    zh = lax.rem(lax.div(seq, 2), N_Z)
    y = lax.div(seq, 2 * N_Z)
    zl = lax.rem(tp, 2)
    x = lax.div(tp, 2)
    d = 1 - 2 * core

    def wrap_y(v):
        return lax.rem(v + 2 * N_Y, N_Y)

    def wrap_z(v):
        return lax.rem(v + 2 * N_Z, N_Z)

    def wrap_x(v):
        return lax.rem(v + 2 * N_X, N_X)

    def at_seq(y_, z_, c_):
        return ((y_ * N_Z + z_) * 2 + c_, tp)

    def at_tp(x_, zl_):
        return (seq, x_ * 2 + zl_)

    partner = at_seq(y, zh, 1 - core)
    next_1 = (lax.rem(seq + 1, N_SEQ), tp)
    next_2 = (lax.rem(seq + 2, N_SEQ), tp)
    prev_1 = (lax.rem(seq + N_SEQ - 1, N_SEQ), tp)
    prev_2 = (lax.rem(seq + N_SEQ - 2, N_SEQ), tp)

    started = []

    def send(src, dst, device):
        n = len(started)
        copy = pltpu.make_async_remote_copy(
            src_ref=src, dst_ref=dst, send_sem=send_sem.at[n], recv_sem=recv_sem.at[n],
            device_id=device, device_id_type=MESH,
        )
        copy.start()
        started.append(copy)
        return copy

    loads = [
        pltpu.make_async_copy(wqkv_h.at[:, pl.ds(QW, 2 * HD)], wkv.at[core, y, zh], local_sem.at[0]),
        pltpu.make_async_copy(wqkv_h.at[:, pl.ds(0, QW)], wq.at[core, y, zh], local_sem.at[1]),
        pltpu.make_async_copy(roll_h, rows, local_sem.at[2]),
        pltpu.make_async_copy(wo_h, wo.at[core, y, zh], local_sem.at[3]),
    ]
    for load in loads:
        load.start()

    barrier = pltpu.get_barrier_semaphore()
    greeted = [partner, next_1, next_2, prev_1, prev_2]
    greeted += [at_seq(y, wrap_z(zh + k), core) for k in range(1, N_Z)]
    greeted += [at_seq(wrap_y(y + k), zh, core) for k in range(1, N_Y)]
    greeted += [(seq, lax.rem(tp + k, N_TP)) for k in range(1, N_TP)]
    for device in greeted:
        pl.semaphore_signal(barrier, inc=1, device_id=device, device_id_type=MESH)
    live_own[...] = jnp.full((8, 128), live_s[0], jnp.int32)
    gain_all = gain_v[...].astype(F32)
    gain_row = lax.broadcasted_iota(jnp.int32, (D // 128, 128), 0)
    gain = jnp.concatenate(
        [
            jnp.sum(jnp.where(gain_row == tp * 5 + i, gain_all, 0.0), axis=0, keepdims=True)
            for i in range(5)
        ],
        axis=1,
    )
    for load in loads:
        load.wait()
    own_a = rows[pl.ds(0, HALF), :].astype(F32)
    acts[tp, pl.ds(0, HALF), :] = (own_a * gain).astype(BF)
    pl.semaphore_wait(barrier, len(greeted))

    up_z = at_seq(y, wrap_z(zh + d), core)
    down_z = at_seq(y, wrap_z(zh - d), core)
    up_y = at_seq(wrap_y(y + d), zh, core)
    down_y = at_seq(wrap_y(y - d), zh, core)
    z_blocks = [zh, wrap_z(zh - d), wrap_z(zh + d), wrap_z(zh + 2 * d)]

    class Gather:
        def __init__(self, buf, first, count):
            self.buf, self.first, self.count = buf, first, count
            self.up, self.down, self.across = {}, {}, []

        def block(self, y_, z_):
            whole = self.count == BLK
            return self.buf.at[core, y_, z_] if whole else (
                self.buf.at[core, y_, z_, pl.ds(self.first, self.count)])

        def line_y(self, y_):
            whole = self.count == BLK
            return self.buf.at[core, y_] if whole else (
                self.buf.at[core, y_, :, pl.ds(self.first, self.count)])

        def line_z(self, z_):
            return self.buf.at[core, :, z_, pl.ds(self.first, self.count)]

        def z_own(self):
            own = self.block(y, zh)
            self.z1, self.z2 = send(own, own, up_z), send(own, own, down_z)

        def z_on(self):
            self.z1.wait_recv()
            held = self.block(y, z_blocks[1])
            self.z3 = send(held, held, up_z)

        def ring(self, b, k):
            if k > 1:
                self.up[b, k - 1].wait_recv()
            held = self.block(wrap_y(y - (k - 1) * d), z_blocks[b])
            self.up[b, k] = send(held, held, up_y)
            if k > 1:
                self.down[b, k - 1].wait_recv()
            if k < 4:
                held = self.block(wrap_y(y + (k - 1) * d), z_blocks[b])
                self.down[b, k] = send(held, held, down_y)

        def step(self, k):
            for b in range(4):
                self.ring(b, k)
            for side in (-(k - 1), k - 1)[: min(k, 2)]:
                held = self.line_y(wrap_y(y + side * d))
                self.across.append(send(held, held, partner))

        def z_arrived(self):
            self.ring(1, 1)
            self.z2.wait_recv()
            self.ring(2, 1)
            self.z3.wait_recv()
            self.ring(3, 1)
            held = self.line_y(y)
            self.across.append(send(held, held, partner))

        def last(self):
            for b in range(4):
                self.up[b, 4].wait_recv()
            held = self.line_y(wrap_y(y + 4))
            self.across.append(send(held, held, partner))

        def column_own(self):
            own = self.line_z(zh)
            self.c1, self.c2 = send(own, own, up_z), send(own, own, down_z)
            self.across.append(send(own, own, partner))

        def column_on(self):
            self.c1.wait_recv()
            held = self.line_z(z_blocks[1])
            self.c3 = send(held, held, up_z)
            self.across.append(send(held, held, partner))

        def column_last(self):
            self.c2.wait_recv()
            held = self.line_z(z_blocks[2])
            self.across.append(send(held, held, partner))
            self.c3.wait_recv()
            held = self.line_z(z_blocks[3])
            self.across.append(send(held, held, partner))

        def wait(self):
            for copy in self.across:
                copy.wait_recv()

    kv = Gather(wkv, 0, BLK)
    qq = Gather(wq, 0, BLK)
    o1 = Gather(wo, 0, O_FIRST)
    o2 = Gather(wo, O_FIRST, BLK - O_FIRST)

    def squares(values):
        total = jnp.sum(values * values, axis=1, keepdims=True)
        return jnp.transpose(jnp.broadcast_to(total, (HALF, 128)))[:8]

    x_up = at_tp(wrap_x(x + 1), zl)
    x_down = at_tp(wrap_x(x - 1), zl)
    z_other = at_tp(x, 1 - zl)

    class Tokens:
        def __init__(self, part):
            self.part = part

        def chunk(self, x_, zl_):
            return acts.at[wrap_x(x_) * 2 + zl_, pl.ds(self.part * HALF, HALF)]

        def own(self):
            own = self.chunk(x, zl)
            self.a = [send(own, own, z_other), send(own, own, x_up), send(own, own, x_down)]

        def second(self):
            self.a[0].wait_recv()
            held = self.chunk(x, 1 - zl)
            self.b = [send(held, held, x_up), send(held, held, x_down)]

        def third(self):
            self.a[1].wait_recv()
            held = self.chunk(x - 1, zl)
            self.c = [send(held, held, x_up)]
            self.b[1].wait_recv()
            held = self.chunk(x + 1, 1 - zl)
            self.c.append(send(held, held, x_down))

        def wait(self):
            for copy in [self.a[2], self.b[0], *self.c]:
                copy.wait_recv()

    tok_a, tok_b = Tokens(0), Tokens(1)

    kv.z_own()
    kv.ring(0, 1)
    live_to_partner = send(live_own, live_p, partner)
    o2.ring(0, 1)
    tok_a.own()
    qq.z_own()
    qq.ring(0, 1)

    row = lax.broadcasted_iota(jnp.int32, (HALF, CAP), 0)
    col = lax.broadcasted_iota(jnp.int32, (HALF, CAP), 1)
    chosen = (col == row + (live_s[0] - HALF)).astype(BF)
    tail_s[...] = jnp.dot(chosen, rows[...], preferred_element_type=F32).astype(BF)
    tail = send(tail_s, tail_r, next_1)
    live_to_partner.wait_recv()
    live_z[0] = live_own[...] + live_p[...]
    live_over_z = [
        send(live_z.at[0], live_z.at[k], at_seq(y, wrap_z(zh + k), core)) for k in range(1, N_Z)
    ]
    ssq[tp, 0] = squares(own_a)

    kv.z_on()
    kv.z_arrived()
    o2.ring(0, 2)
    tok_a.second()
    for copy in live_over_z:
        copy.wait_recv()
    live_y[0] = live_z[0] + live_z[1] + live_z[2] + live_z[3]
    live_over_y = [
        send(live_y.at[0], live_y.at[k], at_seq(wrap_y(y + k), zh, core)) for k in range(1, N_Y)
    ]
    kv.step(2)
    o2.ring(0, 3)
    qq.z_on()
    tok_a.third()
    kv.step(3)
    o2.ring(0, 4)

    for copy in live_over_y:
        copy.wait_recv()
    before = live_p[...] * core - seq * TOK
    for k in range(1, N_Z):
        before = before + live_z[k] * (k <= zh).astype(jnp.int32)
    for k in range(1, N_Y):
        before = before + live_y[k] * (k <= y).astype(jnp.int32)
    spilled = before[:1, :]
    tail.wait_recv()
    row_b = lax.broadcasted_iota(jnp.int32, (HALF, 128), 0)
    keep = jnp.broadcast_to((row_b + spilled < HALF)[:, :1], (HALF, COLS))
    own_b = jnp.where(
        keep, rows[pl.ds(HALF, HALF), :].astype(F32), tail_r[...].astype(F32)
    )
    acts[tp, pl.ds(HALF, HALF), :] = (own_b * gain).astype(BF)
    tok_b.own()
    ssq[tp, 1] = squares(own_b)
    ssq_copies = [
        send(ssq.at[tp], ssq.at[tp], (seq, lax.rem(tp + k, N_TP))) for k in range(1, N_TP)
    ]
    kv.step(4)
    qq.z_arrived()
    tok_b.second()

    position = seq * TOK + lax.broadcasted_iota(jnp.int32, (TOK, 128), 0)
    first = jnp.zeros((TOK, 128), jnp.int32)
    begin = docs_s[0]
    for doc in range(1, 32):
        first = jnp.maximum(first, jnp.where(position >= begin, begin, 0))
        begin = begin + docs_s[doc]
    key_base = [seq, seq - 2, seq - 3 + 2 * core, seq - 1 - 2 * core]
    lane = lax.broadcasted_iota(jnp.int32, (TOK, 128), 1)
    for b in range(4):
        for side in range(2):
            key_pos = key_base[b] * TOK + side * 128 + lane
            allowed = (key_pos <= position) & (key_pos >= first)
            bias[b, :, pl.ds(side * 128, 128)] = jnp.where(allowed, 0.0, NEG)

    o2.up[0, 4].wait_recv()
    o2.column_own()
    kv.last()
    qq.step(2)
    tok_b.third()
    o1.z_own()
    qq.step(3)
    o2.column_on()

    def weight_of(buf, t):
        blocks = []
        for i in range(8):
            s = slot_s[t * 8 + i]
            blocks.append(
                buf[lax.div(s, N_Y * N_Z), lax.rem(lax.div(s, N_Z), N_Y), lax.rem(s, N_Z)]
            )
        return jnp.concatenate(blocks, axis=0)

    def project(buf, total):
        total[...] = jnp.zeros_like(total)

        def one(t, carry):
            total[...] += jnp.dot(acts[t], weight_of(buf, t), preferred_element_type=F32)
            return carry

        lax.fori_loop(0, N_TP, one, 0)

    tok_a.wait()
    tok_b.wait()
    for copy in ssq_copies:
        copy.wait_recv()
    kv.wait()
    project(wkv, acc_kv)

    total = ssq[0]
    for t in range(1, N_TP):
        total = total + ssq[t]
    scale_row = lax.rsqrt(total * (1.0 / D) + EPSILON)
    scale = jnp.concatenate(
        [jnp.transpose(jnp.broadcast_to(scale_row[h, :1], (128, 128))) for h in range(2)], axis=0
    )
    turn_row = lax.broadcasted_iota(jnp.int32, (TOK, TOK), 0)
    turn_col = lax.broadcasted_iota(jnp.int32, (TOK, TOK), 1)
    spilled_wide = jnp.concatenate([spilled, spilled], axis=1)
    turn = (((turn_col - turn_row + spilled_wide + TOK) & (TOK - 1)) == 0).astype(BF)

    def in_order(values):
        return jnp.dot(turn, values, preferred_element_type=F32).astype(BF)

    keys = in_order((acc_kv[:, :HD] * scale).astype(BF))
    values = in_order((acc_kv[:, HD:] * scale).astype(BF))
    kv_own[:, :HD] = keys
    kv_own[:, HD:] = values
    kv_1 = send(kv_own, kv_in.at[0], next_2)
    n_kv = len(started)

    def kv_copy(src):
        return pltpu.make_async_remote_copy(
            src_ref=src, dst_ref=kv_in.at[1], send_sem=send_sem.at[n_kv],
            recv_sem=recv_sem.at[n_kv], device_id=next_1, device_id_type=MESH,
        )

    @pl.when(core == 0)
    def _():
        kv_copy(kv_own).start()

    kv_2 = kv_copy(kv_own)
    started.append(kv_2)
    key_ref[...] = keys
    value_ref[...] = values
    qq.step(4)
    o1.z_on()
    o1.ring(0, 1)
    o1.z_arrived()
    kv_1.wait_recv()

    @pl.when(core == 1)
    def _():
        kv_copy(kv_in.at[0]).start()

    kv_3 = send(kv_in.at[0], kv_in.at[2], partner)
    o2.column_last()
    qq.last()
    o1.step(2)
    qq.wait()
    project(wq, acc_q)
    queries = [
        in_order((acc_q[:, h * HD : (h + 1) * HD] * scale * HD ** (-0.5)).astype(BF))
        for h in range(GROUP)
    ]
    o1.step(3)
    kv_2.wait_recv()
    kv_3.wait_recv()

    pieces = [kv_own, kv_in.at[0], kv_in.at[1], kv_in.at[2]]
    for h in range(GROUP):
        scores = [
            lax.dot_general(
                queries[h], pieces[b][:, :HD], (((1,), (1,)), ((), ())),
                preferred_element_type=F32,
            ) + bias[b]
            for b in range(4)
        ]
        best = jnp.maximum(
            jnp.maximum(scores[0], scores[1]), jnp.maximum(scores[2], scores[3])
        )
        best = jnp.max(best, axis=1, keepdims=True)
        weights = [jnp.exp(s - best) for s in scores]
        totals = jnp.sum(weights[0] + weights[1] + weights[2] + weights[3], axis=1, keepdims=True)
        summed = jnp.dot(weights[0].astype(BF), pieces[0][:, HD:], preferred_element_type=F32)
        for b in range(1, 4):
            summed = summed + jnp.dot(
                weights[b].astype(BF), pieces[b][:, HD:], preferred_element_type=F32
            )
        ctx[:, h * HD : (h + 1) * HD] = (summed / totals).astype(BF)

    o1.step(4)
    o1.last()
    o1.wait()
    o2.wait()

    to_d = at_tp(wrap_x(x + d), zl)
    to_minus_d = at_tp(wrap_x(x - d), zl)
    x_order = [2, d, -d, 0]
    R2 = TOK - R1

    def partial_sum(j, side):
        t = wrap_x(x + x_order[j]) * 2 + (1 - zl if side == 0 else zl)
        part[j, side] = lax.dot_general(
            ctx[...], weight_of(wo, t), (((1,), (1,)), ((), ())), preferred_element_type=F32
        ).astype(BF)

    z1, relay2, direct2, sum2 = {}, {}, {}, {}
    for j in range(4):
        for side in range(2):
            partial_sum(j, side)
            rest = part.at[j, side, pl.ds(R1, R2)]
            if side == 0:
                z1[j] = send(part.at[j, 0, pl.ds(0, R1)], z1_r.at[j], z_other)
            if j == 0:
                relay2[side] = send(rest, x2_r.at[side, 0], to_d)
            if j == 2:
                direct2[side] = send(rest, x2_r.at[side, 1], to_minus_d)

    def rows_1(j):
        return part[j, 1, pl.ds(0, R1), :].astype(F32) + z1_r[j].astype(F32)

    def rows_2(j, side):
        return part[j, side, pl.ds(R1, R2), :].astype(F32)

    z1[0].wait_recv()
    pair_s[0] = rows_1(0).astype(BF)
    relay1 = send(pair_s.at[0], x1_r.at[0], to_d)
    for side in range(2):
        relay2[side].wait_recv()
        sum2_s[side] = (rows_2(1, side) + x2_r[side, 0].astype(F32)).astype(BF)
        sum2[side] = send(sum2_s.at[side], x2_r.at[side, 2], to_d)
    z1[1].wait_recv()
    z1[2].wait_recv()
    pair_s[2] = rows_1(2).astype(BF)
    direct1 = send(pair_s.at[2], x1_r.at[1], to_minus_d)
    relay1.wait_recv()
    pair_s[1] = (rows_1(1) + x1_r[0].astype(F32)).astype(BF)
    sum1 = send(pair_s.at[1], x1_r.at[2], to_d)

    def total_2(side):
        sum2[side].wait_recv()
        direct2[side].wait_recv()
        return rows_2(3, side) + x2_r[side, 1].astype(F32) + x2_r[side, 2].astype(F32)

    z2_s[...] = total_2(0).astype(BF)
    z2 = send(z2_s, z2_r, z_other)
    mine_2 = total_2(1)
    z1[3].wait_recv()
    direct1.wait_recv()
    sum1.wait_recv()
    out_ref[pl.ds(0, R1), :] = (
        rows_1(3) + x1_r[1].astype(F32) + x1_r[2].astype(F32)
    ).astype(BF)
    z2.wait_recv()
    out_ref[pl.ds(R1, R2), :] = (mine_2 + z2_r[...].astype(F32)).astype(BF)
    for copy in started:
        copy.wait_send()


def body(rollout_rows, live_rows, doc_lengths, block_owner, norm_gain, qkv_weight, out_weight):
    positions = jnp.arange(N_SEQ, dtype=jnp.int32)
    slots = lax.rem(positions, 2) * (N_SEQ // 2) + positions // 2
    slot_of = jnp.sum(
        jnp.where(block_owner[None, :] == positions[:, None], slots[None, :], 0), axis=1
    )
    smem = pl.BlockSpec(memory_space=pltpu.SMEM)
    vmem = pl.BlockSpec(memory_space=pltpu.VMEM)
    anyw = pl.BlockSpec(memory_space=pl.ANY)
    V = pltpu.VMEM
    return pl.pallas_call(
        kernel,
        out_shape=(
            jax.ShapeDtypeStruct((TOK, COLS), BF),
            jax.ShapeDtypeStruct((TOK, HD), BF),
            jax.ShapeDtypeStruct((TOK, HD), BF),
        ),
        in_specs=[smem, smem, smem, vmem, anyw, anyw, anyw],
        out_specs=(vmem, vmem, vmem),
        scratch_shapes=[
            V((CAP, COLS), BF),
            V((2, N_Y, N_Z, BLK, 2 * HD), BF),
            V((2, N_Y, N_Z, BLK, QW), BF),
            V((2, N_Y, N_Z, BLK, QW), BF),
            V((N_TP, TOK, COLS), BF),
            V((HALF, COLS), BF),
            V((HALF, COLS), BF),
            V((8, 128), jnp.int32),
            V((8, 128), jnp.int32),
            V((N_Z, 8, 128), jnp.int32),
            V((N_Y, 8, 128), jnp.int32),
            V((N_TP, 2, 8, 128), F32),
            V((TOK, 2 * HD), F32),
            V((TOK, QW), F32),
            V((TOK, 2 * HD), BF),
            V((3, TOK, 2 * HD), BF),
            V((4, TOK, TOK), F32),
            V((TOK, QW), BF),
            V((4, 2, TOK, COLS), BF),
            V((4, R1, COLS), BF),
            V((3, R1, COLS), BF),
            V((3, R1, COLS), BF),
            V((2, 3, TOK - R1, COLS), BF),
            V((2, TOK - R1, COLS), BF),
            V((TOK - R1, COLS), BF),
            V((TOK - R1, COLS), BF),
            pltpu.SemaphoreType.DMA((4,)),
            pltpu.SemaphoreType.DMA((N_COPIES,)),
            pltpu.SemaphoreType.DMA((N_COPIES,)),
        ],
        compiler_params=pltpu.CompilerParams(collective_id=0, has_side_effects=True),
    )(
        live_rows, doc_lengths, slot_of, norm_gain.reshape(D // 128, 128),
        rollout_rows, qkv_weight, out_weight,
    )


def solution(mesh):
    in_specs = (P("seq", "tp"), P("seq"), P(), P(), P(), P("seq", "tp"), P("seq", "tp"))
    out_specs = (P("seq", "tp"), P("seq", "tp"), P("seq", "tp"))
    return jax.shard_map(body, mesh=mesh, in_specs=in_specs, out_specs=out_specs, check_vma=False)
```

time: 141 us -> 117 us (0.83)
  Pallas kernels: 134 us -> 111 us
    pallas_call x1, Pallas kernels: 134 us -> 111 us  [body(): pl.pallas_call(kernel, out_shape=(jax.ShapeDtypeStruct((TOK, COLS), BF),...]
where the time goes in v2:
time: 117 us
  Pallas kernels  111 us (95%)
  local copies, waits for them, and re-layouts  3.89 us (3%)
  between operations  1.31 us (1%)
    pallas_call x1, Pallas kernels, body(): pl.pallas_call(kernel, out_shape=(jax.ShapeDtypeStruct((TOK, COLS), BF),...  111 us
    unnamed x9, local copies, waits for them, and re-layouts  3.89 us

profile of v2, /device:TPU:1, one launch (start us, length us, event | category | flops | bytes accessed | tf_op | source)
XLA Modules:
  0.0 117.1 jit_solution(14091141762480598620)
XLA Ops:
  1.3 0.0 copy-start.2
  1.3 0.6 copy-done.2
  1.9 0.6 select_reduce_fusion.slot_s
  2.6 111.2 %shard_map.94 = (bf16[256,640]{1,0:T(8,128)(2,1)}, bf16[256,128]{1,0:T(8,128)(2,1)}, bf16[256,128]{1,0:T(8,128)(2,1)}) custom-call(s32[1]{0:T(128)S(6)} %copy.13.live_s, s32[32]{0:T(128)} %docs_s.1, s32[64]{0:T(128)} %select_reduce_fusion.slot_s, bf16[40,128]{1,0:T(8,128)(2,1)} %bitcast.1, bf16[384,640]{1,0:T(8,128)(2,1)} %roll_h.1, bf16[80,640]{1,0:T(8,128)(2,1)} %wqkv_h.1, ...), custom_call_target="tpu_custom_call" | custom-call | tf_op jit(solution)/shard_map/pallas_call | solution.py:514
  113.8 0.0 copy-start.1
  113.8 1.8 %copy.14 = bf16[256,640]{1,0:T(8,128)(2,1)} copy(bf16[256,640]{1,0:T(8,128)(2,1)} %get-tuple-element.6) | data formatting | bytes 655360
  115.6 0.0 copy-done.1
  115.6 0.0 copy-start
  115.6 0.6 copy.15
  116.2 0.2 copy-done
  116.4 0.6 copy.16
  (1 shorter events, 0.0 us)
Async XLA Ops:
  1.3 0.7 copy-start.2
  113.8 1.8 %copy-start.1 = (bf16[256,128]{1,0:T(8,128)(2,1)S(1)}, bf16[256,128]{1,0:T(8,128)(2,1)}, u32[]{:S(2)}) copy-start(bf16[256,128]{1,0:T(8,128)(2,1)} %get-tuple-element.7) | copy-start | bytes 196612
  115.6 0.9 copy-start

commit v3 on v2

--- a/solution.py
+++ b/solution.py
@@ -20,7 +20,7 @@
 EPSILON = 1e-06
 NEG = -1e30
 N_COPIES = 200
-O_FIRST = 48
+O_FIRST = 64
 R1 = 112
 MESH = pl.DeviceIdType.MESH
 BF = jnp.bfloat16
@@ -30,7 +30,7 @@
 def kernel(
     live_s, docs_s, slot_s, gain_v, roll_h, wqkv_h, wo_h,
     out_ref, key_ref, value_ref,
-    rows, wkv, wq, wo, acts, tail_s, tail_r, live_own, live_p, live_z, live_y, ssq,
+    rows, wkv, wq, wo, acts, tail_s, tail_r, live_y, live_c, ssq,
     acc_kv, acc_q, kv_own, kv_in, bias, ctx, part,
     z1_r, pair_s, x1_r, x2_r, sum2_s, z2_s, z2_r,
     local_sem, send_sem, recv_sem,
@@ -88,12 +88,12 @@
 
     barrier = pltpu.get_barrier_semaphore()
     greeted = [partner, next_1, next_2, prev_1, prev_2]
-    greeted += [at_seq(y, wrap_z(zh + k), core) for k in range(1, N_Z)]
+    greeted += [at_seq(y, wrap_z(zh + k), c) for k in range(1, N_Z) for c in (core, 1 - core)]
     greeted += [at_seq(wrap_y(y + k), zh, core) for k in range(1, N_Y)]
     greeted += [(seq, lax.rem(tp + k, N_TP)) for k in range(1, N_TP)]
     for device in greeted:
         pl.semaphore_signal(barrier, inc=1, device_id=device, device_id_type=MESH)
-    live_own[...] = jnp.full((8, 128), live_s[0], jnp.int32)
+    live_y[0] = jnp.full((8, 128), live_s[0], jnp.int32)
     gain_all = gain_v[...].astype(F32)
     gain_row = lax.broadcasted_iota(jnp.int32, (D // 128, 128), 0)
     gain = jnp.concatenate(
@@ -107,6 +107,10 @@
         load.wait()
     own_a = rows[pl.ds(0, HALF), :].astype(F32)
     acts[tp, pl.ds(0, HALF), :] = (own_a * gain).astype(BF)
+    row = lax.broadcasted_iota(jnp.int32, (HALF, CAP), 0)
+    col = lax.broadcasted_iota(jnp.int32, (HALF, CAP), 1)
+    chosen = (col == row + (live_s[0] - HALF)).astype(BF)
+    tail_s[...] = jnp.dot(chosen, rows[...], preferred_element_type=F32).astype(BF)
     pl.semaphore_wait(barrier, len(greeted))
 
     up_z = at_seq(y, wrap_z(zh + d), core)
@@ -137,14 +141,17 @@
             own = self.block(y, zh)
             self.z1, self.z2 = send(own, own, up_z), send(own, own, down_z)
 
-        def z_on(self):
-            self.z1.wait_recv()
-            held = self.block(y, z_blocks[1])
-            self.z3 = send(held, held, up_z)
-
         def ring(self, b, k):
             if k > 1:
                 self.up[b, k - 1].wait_recv()
+            elif b == 1:
+                self.z1.wait_recv()
+                held = self.block(y, z_blocks[1])
+                self.z3 = send(held, held, up_z)
+            elif b == 2:
+                self.z2.wait_recv()
+            elif b == 3:
+                self.z3.wait_recv()
             held = self.block(wrap_y(y - (k - 1) * d), z_blocks[b])
             self.up[b, k] = send(held, held, up_y)
             if k > 1:
@@ -153,27 +160,24 @@
                 held = self.block(wrap_y(y + (k - 1) * d), z_blocks[b])
                 self.down[b, k] = send(held, held, down_y)
 
-        def step(self, k):
-            for b in range(4):
-                self.ring(b, k)
-            for side in (-(k - 1), k - 1)[: min(k, 2)]:
-                held = self.line_y(wrap_y(y + side * d))
-                self.across.append(send(held, held, partner))
-
-        def z_arrived(self):
-            self.ring(1, 1)
-            self.z2.wait_recv()
-            self.ring(2, 1)
-            self.z3.wait_recv()
-            self.ring(3, 1)
-            held = self.line_y(y)
+        def line_across(self, y_):
+            held = self.line_y(wrap_y(y_))
             self.across.append(send(held, held, partner))
+
+        def wave(self, w):
+            for b, later in enumerate((0, 1, 1, 2)):
+                if 1 <= w - later <= 4:
+                    self.ring(b, w - later)
+            if w == 3:
+                self.line_across(y)
+            elif w > 3:
+                self.line_across(y - (w - 3) * d)
+                self.line_across(y + (w - 3) * d)
 
         def last(self):
             for b in range(4):
                 self.up[b, 4].wait_recv()
-            held = self.line_y(wrap_y(y + 4))
-            self.across.append(send(held, held, partner))
+            self.line_across(y + 4)
 
         def column_own(self):
             own = self.line_z(zh)
@@ -241,50 +245,47 @@
 
     tok_a, tok_b = Tokens(0), Tokens(1)
 
-    kv.z_own()
-    kv.ring(0, 1)
-    live_to_partner = send(live_own, live_p, partner)
-    o2.ring(0, 1)
-    tok_a.own()
-    qq.z_own()
-    qq.ring(0, 1)
-
-    row = lax.broadcasted_iota(jnp.int32, (HALF, CAP), 0)
-    col = lax.broadcasted_iota(jnp.int32, (HALF, CAP), 1)
-    chosen = (col == row + (live_s[0] - HALF)).astype(BF)
-    tail_s[...] = jnp.dot(chosen, rows[...], preferred_element_type=F32).astype(BF)
-    tail = send(tail_s, tail_r, next_1)
-    live_to_partner.wait_recv()
-    live_z[0] = live_own[...] + live_p[...]
-    live_over_z = [
-        send(live_z.at[0], live_z.at[k], at_seq(y, wrap_z(zh + k), core)) for k in range(1, N_Z)
-    ]
-    ssq[tp, 0] = squares(own_a)
-
-    kv.z_on()
-    kv.z_arrived()
-    o2.ring(0, 2)
-    tok_a.second()
-    for copy in live_over_z:
-        copy.wait_recv()
-    live_y[0] = live_z[0] + live_z[1] + live_z[2] + live_z[3]
     live_over_y = [
         send(live_y.at[0], live_y.at[k], at_seq(wrap_y(y + k), zh, core)) for k in range(1, N_Y)
     ]
-    kv.step(2)
-    o2.ring(0, 3)
-    qq.z_on()
-    tok_a.third()
-    kv.step(3)
-    o2.ring(0, 4)
-
+    kv.z_own()
+    kv.wave(1)
+    qq.z_own()
+    qq.wave(1)
+    tok_a.own()
+    o2.ring(0, 1)
+    tail = send(tail_s, tail_r, next_1)
+    ssq[tp, 0] = squares(own_a)
+    kv.wave(2)
     for copy in live_over_y:
         copy.wait_recv()
-    before = live_p[...] * core - seq * TOK
-    for k in range(1, N_Z):
-        before = before + live_z[k] * (k <= zh).astype(jnp.int32)
+    earlier = jnp.zeros((8, 128), jnp.int32)
     for k in range(1, N_Y):
-        before = before + live_y[k] * (k <= y).astype(jnp.int32)
+        earlier = earlier + live_y[k] * (k <= y).astype(jnp.int32)
+    live_c[0, 0] = earlier
+    live_c[0, 1] = live_y[0]
+    live_over_z = [
+        send(
+            live_c.at[0], live_c.at[n],
+            at_seq(y, wrap_z(zh + n // 2), 1 - core if n % 2 else core),
+        )
+        for n in range(1, 2 * N_Z)
+    ]
+    o2.ring(0, 2)
+    qq.wave(2)
+    tok_a.second()
+    kv.wave(3)
+    o2.ring(0, 3)
+    qq.wave(3)
+    tok_a.third()
+    o1.z_own()
+
+    for copy in live_over_z:
+        copy.wait_recv()
+    before = live_c[0, 0] - seq * TOK
+    for n in range(1, 2 * N_Z):
+        counts = core if n == 1 else (n // 2 <= zh).astype(jnp.int32)
+        before = before + live_c[n, 0] + live_c[n, 1] * counts
     spilled = before[:1, :]
     tail.wait_recv()
     row_b = lax.broadcasted_iota(jnp.int32, (HALF, 128), 0)
@@ -298,9 +299,13 @@
     ssq_copies = [
         send(ssq.at[tp], ssq.at[tp], (seq, lax.rem(tp + k, N_TP))) for k in range(1, N_TP)
     ]
-    kv.step(4)
-    qq.z_arrived()
+    kv.wave(4)
+    o2.ring(0, 4)
+    qq.wave(4)
     tok_b.second()
+    o2.up[0, 4].wait_recv()
+    o2.column_own()
+    kv.wave(5)
 
     position = seq * TOK + lax.broadcasted_iota(jnp.int32, (TOK, 128), 0)
     first = jnp.zeros((TOK, 128), jnp.int32)
@@ -316,14 +321,15 @@
             allowed = (key_pos <= position) & (key_pos >= first)
             bias[b, :, pl.ds(side * 128, 128)] = jnp.where(allowed, 0.0, NEG)
 
-    o2.up[0, 4].wait_recv()
-    o2.column_own()
+    qq.wave(5)
+    tok_b.third()
+    o1.wave(1)
+    o2.column_on()
+    kv.wave(6)
     kv.last()
-    qq.step(2)
-    tok_b.third()
-    o1.z_own()
-    qq.step(3)
-    o2.column_on()
+    qq.wave(6)
+    o1.wave(2)
+    o1.wave(3)
 
     def weight_of(buf, t):
         blocks = []
@@ -386,27 +392,24 @@
     started.append(kv_2)
     key_ref[...] = keys
     value_ref[...] = values
-    qq.step(4)
-    o1.z_on()
-    o1.ring(0, 1)
-    o1.z_arrived()
-    kv_1.wait_recv()
-
-    @pl.when(core == 1)
-    def _():
-        kv_copy(kv_in.at[0]).start()
-
-    kv_3 = send(kv_in.at[0], kv_in.at[2], partner)
-    o2.column_last()
     qq.last()
-    o1.step(2)
+    o1.wave(4)
     qq.wait()
     project(wq, acc_q)
     queries = [
         in_order((acc_q[:, h * HD : (h + 1) * HD] * scale * HD ** (-0.5)).astype(BF))
         for h in range(GROUP)
     ]
-    o1.step(3)
+    kv_1.wait_recv()
+
+    @pl.when(core == 1)
+    def _():
+        kv_copy(kv_in.at[0]).start()
+
+    kv_3 = send(kv_in.at[0], kv_in.at[2], partner)
+    o1.wave(5)
+    o2.column_last()
+    o1.wave(6)
     kv_2.wait_recv()
     kv_3.wait_recv()
 
@@ -432,7 +435,6 @@
             )
         ctx[:, h * HD : (h + 1) * HD] = (summed / totals).astype(BF)
 
-    o1.step(4)
     o1.last()
     o1.wait()
     o2.wait()
@@ -528,10 +530,8 @@
             V((N_TP, TOK, COLS), BF),
             V((HALF, COLS), BF),
             V((HALF, COLS), BF),
-            V((8, 128), jnp.int32),
-            V((8, 128), jnp.int32),
-            V((N_Z, 8, 128), jnp.int32),
             V((N_Y, 8, 128), jnp.int32),
+            V((2 * N_Z, 2, 8, 128), jnp.int32),
             V((N_TP, 2, 8, 128), F32),
             V((TOK, 2 * HD), F32),
             V((TOK, QW), F32),

time: 117 us -> 110 us (0.940)
  Pallas kernels: 111 us -> 104 us
    pallas_call x1, Pallas kernels: 111 us -> 104 us  [body(): pl.pallas_call(kernel, out_shape=(jax.ShapeDtypeStruct((TOK, COLS), BF),...]
where the time goes in v3:
time: 110 us
  Pallas kernels  104 us (95%)
  local copies, waits for them, and re-layouts  3.89 us (4%)
  between operations  1.31 us (1%)
    pallas_call x1, Pallas kernels, body(): pl.pallas_call(kernel, out_shape=(jax.ShapeDtypeStruct((TOK, COLS), BF),...  104 us
    unnamed x9, local copies, waits for them, and re-layouts  3.89 us

profile of v3, /device:TPU:1, one launch (start us, length us, event | category | flops | bytes accessed | tf_op | source)
XLA Modules:
  0.0 109.8 jit_solution(18068149087941574292)
XLA Ops:
  1.3 0.0 copy-start.2
  1.3 0.6 copy-done.2
  1.9 0.6 select_reduce_fusion.slot_s
  2.6 104.0 %shard_map.94 = (bf16[256,640]{1,0:T(8,128)(2,1)}, bf16[256,128]{1,0:T(8,128)(2,1)}, bf16[256,128]{1,0:T(8,128)(2,1)}) custom-call(s32[1]{0:T(128)S(6)} %copy.13.live_s, s32[32]{0:T(128)} %docs_s.1, s32[64]{0:T(128)} %select_reduce_fusion.slot_s, bf16[40,128]{1,0:T(8,128)(2,1)} %bitcast.1, bf16[384,640]{1,0:T(8,128)(2,1)} %roll_h.1, bf16[80,640]{1,0:T(8,128)(2,1)} %wqkv_h.1, ...), custom_call_target="tpu_custom_call" | custom-call | tf_op jit(solution)/shard_map/pallas_call | solution.py:516
  106.6 0.0 copy-start.1
  106.6 1.8 %copy.14 = bf16[256,640]{1,0:T(8,128)(2,1)} copy(bf16[256,640]{1,0:T(8,128)(2,1)} %get-tuple-element.6) | data formatting | bytes 655360
  108.3 0.0 copy-done.1
  108.4 0.0 copy-start
  108.4 0.6 copy.15
  109.0 0.2 copy-done
  109.2 0.6 copy.16
  (1 shorter events, 0.0 us)
Async XLA Ops:
  1.3 0.7 copy-start.2
  106.6 1.8 %copy-start.1 = (bf16[256,128]{1,0:T(8,128)(2,1)S(1)}, bf16[256,128]{1,0:T(8,128)(2,1)}, u32[]{:S(2)}) copy-start(bf16[256,128]{1,0:T(8,128)(2,1)} %get-tuple-element.7) | copy-start | bytes 196612
  108.4 0.9 copy-start

commit v4 on v3

--- a/solution.py
+++ b/solution.py
@@ -28,10 +28,10 @@
 
 
 def kernel(
-    live_s, docs_s, slot_s, gain_v, roll_h, wqkv_h, wo_h,
+    live_s, docs_s, owner_s, gain_v, roll_h, wqkv_h, wo_h,
     out_ref, key_ref, value_ref,
     rows, wkv, wq, wo, acts, tail_s, tail_r, live_y, live_c, ssq,
-    acc_kv, acc_q, kv_own, kv_in, bias, ctx, part,
+    slot_v, slot_s, acc_kv, acc_q, kv_own, kv_in, bias, ctx, part,
     z1_r, pair_s, x1_r, x2_r, sum2_s, z2_s, z2_r,
     local_sem, send_sem, recv_sem,
 ):
@@ -94,6 +94,11 @@
     for device in greeted:
         pl.semaphore_signal(barrier, inc=1, device_id=device, device_id_type=MESH)
     live_y[0] = jnp.full((8, 128), live_s[0], jnp.int32)
+    block = lax.broadcasted_iota(jnp.int32, (8, 128), 1)
+    place = jnp.zeros((8, 128), jnp.int32)
+    for j in range(N_SEQ):
+        place = jnp.where(block == owner_s[j], (j % 2) * (N_SEQ // 2) + j // 2, place)
+    slot_v[...] = place
     gain_all = gain_v[...].astype(F32)
     gain_row = lax.broadcasted_iota(jnp.int32, (D // 128, 128), 0)
     gain = jnp.concatenate(
@@ -111,6 +116,8 @@
     col = lax.broadcasted_iota(jnp.int32, (HALF, CAP), 1)
     chosen = (col == row + (live_s[0] - HALF)).astype(BF)
     tail_s[...] = jnp.dot(chosen, rows[...], preferred_element_type=F32).astype(BF)
+    slots = pltpu.make_async_copy(slot_v, slot_s, local_sem.at[4])
+    slots.start()
     pl.semaphore_wait(barrier, len(greeted))
 
     up_z = at_seq(y, wrap_z(zh + d), core)
@@ -326,15 +333,15 @@
     o1.wave(1)
     o2.column_on()
     kv.wave(6)
-    kv.last()
     qq.wave(6)
     o1.wave(2)
+    kv.last()
     o1.wave(3)
 
     def weight_of(buf, t):
         blocks = []
         for i in range(8):
-            s = slot_s[t * 8 + i]
+            s = slot_s[0, t * 8 + i]
             blocks.append(
                 buf[lax.div(s, N_Y * N_Z), lax.rem(lax.div(s, N_Z), N_Y), lax.rem(s, N_Z)]
             )
@@ -349,6 +356,7 @@
 
         lax.fori_loop(0, N_TP, one, 0)
 
+    slots.wait()
     tok_a.wait()
     tok_b.wait()
     for copy in ssq_copies:
@@ -400,6 +408,7 @@
         in_order((acc_q[:, h * HD : (h + 1) * HD] * scale * HD ** (-0.5)).astype(BF))
         for h in range(GROUP)
     ]
+    o1.wave(5)
     kv_1.wait_recv()
 
     @pl.when(core == 1)
@@ -407,9 +416,9 @@
         kv_copy(kv_in.at[0]).start()
 
     kv_3 = send(kv_in.at[0], kv_in.at[2], partner)
-    o1.wave(5)
+    o1.wave(6)
     o2.column_last()
-    o1.wave(6)
+    o1.last()
     kv_2.wait_recv()
     kv_3.wait_recv()
 
@@ -435,7 +444,6 @@
             )
         ctx[:, h * HD : (h + 1) * HD] = (summed / totals).astype(BF)
 
-    o1.last()
     o1.wait()
     o2.wait()
 
@@ -504,11 +512,6 @@
 
 
 def body(rollout_rows, live_rows, doc_lengths, block_owner, norm_gain, qkv_weight, out_weight):
-    positions = jnp.arange(N_SEQ, dtype=jnp.int32)
-    slots = lax.rem(positions, 2) * (N_SEQ // 2) + positions // 2
-    slot_of = jnp.sum(
-        jnp.where(block_owner[None, :] == positions[:, None], slots[None, :], 0), axis=1
-    )
     smem = pl.BlockSpec(memory_space=pltpu.SMEM)
     vmem = pl.BlockSpec(memory_space=pltpu.VMEM)
     anyw = pl.BlockSpec(memory_space=pl.ANY)
@@ -516,9 +519,9 @@
     return pl.pallas_call(
         kernel,
         out_shape=(
-            jax.ShapeDtypeStruct((TOK, COLS), BF),
-            jax.ShapeDtypeStruct((TOK, HD), BF),
-            jax.ShapeDtypeStruct((TOK, HD), BF),
+            pltpu.VMEM((TOK, COLS), BF),
+            pltpu.VMEM((TOK, HD), BF),
+            pltpu.VMEM((TOK, HD), BF),
         ),
         in_specs=[smem, smem, smem, vmem, anyw, anyw, anyw],
         out_specs=(vmem, vmem, vmem),
@@ -533,6 +536,8 @@
             V((N_Y, 8, 128), jnp.int32),
             V((2 * N_Z, 2, 8, 128), jnp.int32),
             V((N_TP, 2, 8, 128), F32),
+            V((8, 128), jnp.int32),
+            pltpu.SMEM((8, 128), jnp.int32),
             V((TOK, 2 * HD), F32),
             V((TOK, QW), F32),
             V((TOK, 2 * HD), BF),
@@ -547,13 +552,13 @@
             V((2, TOK - R1, COLS), BF),
             V((TOK - R1, COLS), BF),
             V((TOK - R1, COLS), BF),
-            pltpu.SemaphoreType.DMA((4,)),
+            pltpu.SemaphoreType.DMA((5,)),
             pltpu.SemaphoreType.DMA((N_COPIES,)),
             pltpu.SemaphoreType.DMA((N_COPIES,)),
         ],
         compiler_params=pltpu.CompilerParams(collective_id=0, has_side_effects=True),
     )(
-        live_rows, doc_lengths, slot_of, norm_gain.reshape(D // 128, 128),
+        live_rows, doc_lengths, block_owner, norm_gain.reshape(D // 128, 128),
         rollout_rows, qkv_weight, out_weight,
     )
 

time: 110 us -> 104 us (0.945); the launches traced: 110 us -> 103 us
  Pallas kernels: 104 us -> 99.3 us
  local copies, waits for them, and re-layouts: 3.89 us -> 1.98 us
    pallas_call x1, Pallas kernels: 104 us -> 99.3 us  [body(): pl.pallas_call(kernel, out_shape=(pltpu.VMEM((TOK, COLS), BF), pltpu.VMEM...]
    unnamed x9 -> x3, local copies, waits for them, and re-layouts: 3.89 us -> 1.98 us
where the time goes in v4:
time: 104 us; the launch traced here: 103 us
  Pallas kernels  99.3 us (95%)
  local copies, waits for them, and re-layouts  1.98 us (2%)
  between operations  1.29 us (1%)
    pallas_call x1, Pallas kernels, body(): pl.pallas_call(kernel, out_shape=(pltpu.VMEM((TOK, COLS), BF), pltpu.VMEM...  99.3 us

profile of v4, /device:TPU:1, one launch (start us, length us, event | category | flops | bytes accessed | tf_op | source)
XLA Modules:
  0.0 102.6 jit_solution(8534802268162019288)
XLA Ops:
  1.3 99.3 %shard_map.94 = (bf16[256,640]{1,0:T(8,128)(2,1)S(1)}, bf16[256,128]{1,0:T(8,128)(2,1)S(1)}, bf16[256,128]{1,0:T(8,128)(2,1)S(1)}) custom-call(s32[1]{0:T(128)S(6)} %copy.16.live_s, s32[32]{0:T(128)} %docs_s.1, s32[64]{0:T(128)} %owner_s.1, bf16[40,128]{1,0:T(8,128)(2,1)} %bitcast.1, bf16[384,640]{1,0:T(8,128)(2,1)} %roll_h.1, bf16[80,640]{1,0:T(8,128)(2,1)} %wqkv_h.1, ...), custom_call_target="tpu_custom_call" | custom-call | tf_op jit(solution)/shard_map/pallas_call | solution.py:519
  100.6 0.7 copy.13
  101.4 0.6 copy.14
  102.0 0.6 copy.15

commit v5 on v4

--- a/solution.py
+++ b/solution.py
@@ -263,6 +263,21 @@
     o2.ring(0, 1)
     tail = send(tail_s, tail_r, next_1)
     ssq[tp, 0] = squares(own_a)
+
+    position = seq * TOK + lax.broadcasted_iota(jnp.int32, (TOK, 128), 0)
+    first = jnp.zeros((TOK, 128), jnp.int32)
+    begin = docs_s[0]
+    for doc in range(1, 32):
+        first = jnp.maximum(first, jnp.where(position >= begin, begin, 0))
+        begin = begin + docs_s[doc]
+    key_base = [seq, seq - 2, seq - 3 + 2 * core, seq - 1 - 2 * core]
+    lane = lax.broadcasted_iota(jnp.int32, (TOK, 128), 1)
+    for b in range(4):
+        for side in range(2):
+            key_pos = key_base[b] * TOK + side * 128 + lane
+            allowed = (key_pos <= position) & (key_pos >= first)
+            bias[b, :, pl.ds(side * 128, 128)] = jnp.where(allowed, 0.0, NEG)
+
     kv.wave(2)
     for copy in live_over_y:
         copy.wait_recv()
@@ -313,21 +328,6 @@
     o2.up[0, 4].wait_recv()
     o2.column_own()
     kv.wave(5)
-
-    position = seq * TOK + lax.broadcasted_iota(jnp.int32, (TOK, 128), 0)
-    first = jnp.zeros((TOK, 128), jnp.int32)
-    begin = docs_s[0]
-    for doc in range(1, 32):
-        first = jnp.maximum(first, jnp.where(position >= begin, begin, 0))
-        begin = begin + docs_s[doc]
-    key_base = [seq, seq - 2, seq - 3 + 2 * core, seq - 1 - 2 * core]
-    lane = lax.broadcasted_iota(jnp.int32, (TOK, 128), 1)
-    for b in range(4):
-        for side in range(2):
-            key_pos = key_base[b] * TOK + side * 128 + lane
-            allowed = (key_pos <= position) & (key_pos >= first)
-            bias[b, :, pl.ds(side * 128, 128)] = jnp.where(allowed, 0.0, NEG)
-
     qq.wave(5)
     tok_b.third()
     o1.wave(1)

time: 104 us -> 104 us (level)
  no operation moved by 1% of the time
where the time goes in v5:
time: 104 us; the launch traced here: 103 us
  Pallas kernels  99.3 us (95%)
  local copies, waits for them, and re-layouts  1.98 us (2%)
  between operations  1.29 us (1%)
    pallas_call x1, Pallas kernels, body(): pl.pallas_call(kernel, out_shape=(pltpu.VMEM((TOK, COLS), BF), pltpu.VMEM...  99.3 us

profile of v5, /device:TPU:1, one launch (start us, length us, event | category | flops | bytes accessed | tf_op | source)
XLA Modules:
  0.0 102.6 jit_solution(10859869932718827186)
XLA Ops:
  1.3 99.3 %shard_map.94 = (bf16[256,640]{1,0:T(8,128)(2,1)S(1)}, bf16[256,128]{1,0:T(8,128)(2,1)S(1)}, bf16[256,128]{1,0:T(8,128)(2,1)S(1)}) custom-call(s32[1]{0:T(128)S(6)} %copy.16.live_s, s32[32]{0:T(128)} %docs_s.1, s32[64]{0:T(128)} %owner_s.1, bf16[40,128]{1,0:T(8,128)(2,1)} %bitcast.1, bf16[384,640]{1,0:T(8,128)(2,1)} %roll_h.1, bf16[80,640]{1,0:T(8,128)(2,1)} %wqkv_h.1, ...), custom_call_target="tpu_custom_call" | custom-call | tf_op jit(solution)/shard_map/pallas_call | solution.py:519
  100.6 0.7 copy.13
  101.4 0.6 copy.14
  102.0 0.6 copy.15
